TPU v7x, 32 devices: a whole 2x2x4 slice. The times are simulated.
32 devices in a mesh: cls: 8 (over z, y), row: 4 (over x, core).
Axes of the slice: x: 2, y: 2, z: 4, core: 2. Of those that a mesh axis runs over, the one named last changes fastest.
Arguments:
- embeddings: float32 [1024, 1024], P('row'), may hold values from -6 to 6
- weights: float32 [1024, 81920], P(('cls', 'row')), may hold values from -4 to 4
- labels: int32 [1024], replicated, may hold values from 0 to 81919, as said below
Outputs:
- weight_update: float32 [1024, 81920], P(None, ('cls', 'row'))
- losses: float32 [2, 1024], replicated
Inputs may be any that keep to these rules, and one draw needn't show every extreme that they name: labels take at most 512 distinct values, at most one in each aligned run of 160 classes; rows may share a label.
All inputs are finite; a program needn't handle non-finite values.
Results may differ from a plain program's by a relative error of at most 0.012.
The roundings to bfloat16 on the way count: a program that leaves them out, or rounds other values in their place, can miss the bound.
Values may be sent and summed in bfloat16 or wider, within the bound.
No kernel may reach another device: no remote copies, remote signals or barrier semaphores. Data moves between devices by JAX's collectives and lax.ppermute only.
A program may use at most 128 MiB of HBM per device.

v0:
```python
import jax
import jax.numpy as jnp
from jax import lax
from jax.sharding import PartitionSpec as P

STEPS = 2
learn_rate = 2.0


def shards(embeddings, weights, labels):
    peer_count = lax.axis_size(("cls", "row"))
    examples = lax.all_gather(embeddings.astype(jnp.bfloat16), "row", axis=0, tiled=True)
    row_count = examples.shape[0]
    feature_rows = weights.shape[0]
    class_count = weights.shape[1] // peer_count
    model_width = feature_rows * peer_count
    offset = lax.axis_index(("cls", "row")) * class_count
    columns = lax.broadcasted_iota(jnp.int32, (1, class_count), 1) + offset
    label_hit = columns == labels[:, None]
    pieces = weights.reshape(feature_rows, peer_count, class_count // 128, 128)
    block_weights = lax.all_to_all(pieces, ("cls", "row"), split_axis=1, concat_axis=0, tiled=True)[
        :, 0
    ]
    block_width = block_weights.shape[1] * 128
    flat_weights = block_weights.reshape(block_weights.shape[0], block_width)
    block_logits = jnp.dot(
        examples, flat_weights.astype(jnp.bfloat16), preferred_element_type=jnp.float32
    )
    first_logits = block_logits.reshape(row_count, block_weights.shape[1], 128)
    current = block_weights.reshape(model_width, class_count)
    logits = first_logits.reshape(row_count, class_count)
    starting = current
    loss_rows = []
    for step_index in range(STEPS):
        if step_index > 0:
            logits = jnp.dot(
                examples, current.astype(jnp.bfloat16), preferred_element_type=jnp.float32
            )
        local_peak = jnp.max(logits, axis=1)
        local_picked = jnp.sum(jnp.where(label_hit, logits, 0.0), axis=1)
        row_peak = lax.pmax(local_peak, ("cls", "row"))
        row_total, picked = lax.psum(
            (jnp.sum(jnp.exp(logits - row_peak[:, None]), axis=1), local_picked), ("cls", "row")
        )
        log_norm = row_peak + jnp.log(row_total)
        loss_rows.append(log_norm - picked)
        onehot = jnp.where(label_hit, 1.0, 0.0)
        residual = (jnp.exp(logits - log_norm[:, None]) - onehot).astype(jnp.bfloat16)
        gradient = (
            lax.dot_general(
                examples, residual, (((0,), (0,)), ((), ())), preferred_element_type=jnp.float32
            )
            / row_count
        )
        current = current - learn_rate * gradient
    return (current - starting, jnp.stack(loss_rows))


def solution(mesh):
    placed = (P("row", None), P(("cls", "row"), None), P())
    return jax.shard_map(
        shards,
        mesh=mesh,
        in_specs=placed,
        out_specs=(P(None, ("cls", "row")), P()),
        check_vma=False,
    )
```

profile of v0, /device:TPU:0, one launch (start us, length us, event | category | flops | bytes accessed | tf_op | source)
XLA Modules:
  0.0 578.8 jit_solution(8699041707677321800)
XLA Ops:
  7.2 9.4 %reshape.18 = f32[32,32,20,128]{3,2,1,0:T(8,128)} reshape(f32[32,81920]{1,0:T(8,128)} %param.4) | data formatting | bytes 20971520 | tf_op jit(solution)/shard_map/reshape | solution.py:20
  16.6 14.7 %copy.13 = f32[32,32,20,128]{3,0,2,1:T(8,128)} copy(f32[32,32,20,128]{3,2,1,0:T(8,128)} %reshape.18) | data formatting | bytes 20971520 | tf_op jit(solution)/shard_map/reshape | solution.py:20
  31.3 7.4 %all-to-all-start = ((f32[32,32,20,128]{3,0,2,1:T(8,128)}), f32[32,32,20,128]{3,0,2,1:T(8,128)}, u32[]{:S(2)}, u32[]{:S(2)}) async-start(f32[32,32,20,128]{3,0,2,1:T(8,128)} %copy.13), calls=%async_computation | async-start | bytes 20971520 | tf_op jit(solution)/shard_map/all_to_all | solution.py:21
  38.8 0.4 all-gather.2.cloned.1.call-start
  39.2 0.0 copy-done
  39.2 0.9 convert_element_type.15
  40.1 0.0 all-gather.2.cloned.1.call-update
  40.1 234.6 %all-to-all-done = f32[32,32,20,128]{3,0,2,1:T(8,128)} async-done(((f32[32,32,20,128]{3,0,2,1:T(8,128)}), f32[32,32,20,128]{3,0,2,1:T(8,128)}, u32[]{:S(2)}, u32[]{:S(2)}) %all-to-all-start) | async-done | bytes 10485792 | tf_op jit(solution)/shard_map/all_to_all | solution.py:21
  274.7 17.8 %copy.14 = f32[32,32,1,20,128]{4,3,1,0,2:T(8,128)} copy(f32[32,32,1,20,128]{4,1,3,0,2:T(8,128)} %bitcast.1) | data formatting | bytes 20971520 | tf_op jit(solution)/shard_map/all_to_all | solution.py:21
  292.5 21.9 %copy.21 = f32[128,8,20,128]{3,1,2,0:T(8,128)} copy(f32[128,8,20,128]{3,2,1,0:T(8,128)} %bitcast.41) | data formatting | bytes 20971520
  314.4 11.4 %copy.15 = f32[1024,2560]{0,1:T(8,128)} copy(f32[1024,2560]{1,0:T(8,128)} %bitcast.42) | data formatting | bytes 20971520 | tf_op jit(solution)/shard_map/reshape;squeeze | solution.py:30
  325.8 11.4 %fusion.35 = (f32[1024]{0:T(1024)S(1)}, f32[1024,2560]{1,0:T(8,128)}) fusion(bf16[1024,1024]{1,0:T(8,128)(2,1)} %all-gather.2.cloned.1.call-done, f32[1024,2560]{1,0:T(8,128)} %bitcast.43), kind=kOutput, calls=%fused_computation.45 | convolution fusion | flops 5373950976 | bytes 23072768 | tf_op jit(solution)/shard_map/dot_general | solution.py:26
  337.2 36.8 %pmax.14 = f32[1024]{0:T(1024)S(1)} all-reduce(f32[1024]{0:T(1024)S(1)} %get-tuple-element.17), channel_id=1, replica_groups=mesh['cls'=8,'row'=4] {'cls','row'}, use_global_device_ids=true, to_apply=%region_1.2 | all-reduce | flops 1024 | bytes 8192 | tf_op jit(solution)/shard_map/pmax | solution.py:41
  374.0 5.7 fusion.4
  379.7 41.0 %psum.28 = f32[1024]{0:T(1024)S(1)} all-reduce(f32[1024]{0:T(1024)S(1)} %get-tuple-element.9), channel_id=1, replica_groups=mesh['cls'=8,'row'=4] {'cls','row'}, use_global_device_ids=true, to_apply=%region_3.4 | all-reduce | flops 1024 | bytes 8192 | tf_op jit(solution)/shard_map/psum | solution.py:42
  420.7 12.0 %fusion.14 = f32[2560,1024]{1,0:T(8,128)} fusion(bf16[1024,1024]{1,0:T(8,128)(2,1)} %all-gather.2.cloned.1.call-done, f32[1024,2560]{1,0:T(8,128)} %get-tuple-element.18, s32[2560]{0:T(1024)S(1)} %iota_add_fusion, f32[1024]{0:T(1024)S(1)} %log_add_fusion.1, s32[1024]{0:T(1024)S(1)} %copy-done.1), kind=kOutput, calls=%fused_computation.21 | convolution fusion | flops 5381816320 | bytes 23087104 | tf_op jit(solution)/shard_map/dot_general | solution.py:50
  432.8 12.4 %fusion.36 = (f32[1024]{0:T(1024)S(1)}, f32[2560,1024]{1,0:T(8,128)}) fusion(bf16[1024,1024]{1,0:T(8,128)(2,1)S(1)} %copy-done.2, f32[1024,2560]{0,1:T(8,128)S(1)} %bitcast.45, f32[2560,1024]{1,0:T(8,128)} %fusion.14), kind=kOutput, calls=%fused_computation.46 | convolution fusion | flops 5379193856 | bytes 33558528 | tf_op jit(solution)/shard_map/dot_general | solution.py:36
  445.2 39.6 %pmax.15 = f32[1024]{0:T(1024)S(1)} all-reduce(f32[1024]{0:T(1024)S(1)} %get-tuple-element.19), channel_id=1, replica_groups=mesh['cls'=8,'row'=4] {'cls','row'}, use_global_device_ids=true, to_apply=%region_5.6 | all-reduce | flops 1024 | bytes 8192 | tf_op jit(solution)/shard_map/pmax | solution.py:41
  484.8 11.5 %copy.16 = f32[2560,1024]{0,1:T(8,128)} copy(f32[2560,1024]{1,0:T(8,128)} %get-tuple-element.20) | data formatting | bytes 20971520 | tf_op jit(solution)/shard_map/dot_general | solution.py:36
  496.3 5.6 fusion.5
  501.9 40.6 %all-reduce = (f32[1024]{0:T(1024)S(1)}, f32[1024]{0:T(1024)S(1)}, f32[1024]{0:T(1024)S(1)}) all-reduce(f32[1024]{0:T(1024)S(1)} %get-tuple-element.11, f32[1024]{0:T(1024)S(1)} %get-tuple-element.10, f32[1024]{0:T(1024)S(1)} %get-tuple-element.8), channel_id=1, replica_groups=mesh['cls'=8,'row'=4] {'cls','row'}, use_global_device_ids=true, to_apply=%region_7.8 | all-reduce | flops 3072 | bytes 24576 | tf_op jit(solution)/shard_map/psum | solution.py:42
  542.5 17.2 %fusion.6 = f32[1024,2560]{0,1:T(8,128)} fusion(f32[1024,2560]{0,1:T(8,128)} %copy.15, f32[2560,1024]{1,0:T(8,128)} %fusion.14, bf16[1024,1024]{1,0:T(8,128)(2,1)} %all-gather.2.cloned.1.call-done, f32[2560,1024]{0,1:T(8,128)} %copy.16, f32[1024]{0:T(1024)S(1)} %get-tuple-element.16, s32[2560]{0:T(1024)S(1)} %iota_add_fusion, s32[1024]{0:T(1024)S(1)} %copy-done.1), kind=kOutput, calls=%fused_computation.11 | convolution fusion | flops 5394923520 | bytes 44058624 | tf_op jit(solution)/shard_map/dot_general | solution.py:50
  559.7 11.4 %copy.18 = f32[1024,2560]{1,0:T(8,128)} copy(f32[1024,2560]{0,1:T(8,128)} %fusion.6) | data formatting | bytes 20971520
  571.1 0.6 pad_maximum_fusion
  (17 shorter events, 0.0 us)
Async XLA Ops:
  31.3 7.9 %copy-start = (f32[256,1024]{1,0:T(8,128)S(1)}, f32[256,1024]{1,0:T(8,128)}, u32[]{:S(2)}) copy-start(f32[256,1024]{1,0:T(8,128)} %param.3) | copy-start | bytes 3145732
  31.3 243.4 %all-to-all-start = ((f32[32,32,20,128]{3,0,2,1:T(8,128)}), f32[32,32,20,128]{3,0,2,1:T(8,128)}, u32[]{:S(2)}, u32[]{:S(2)}) async-start(f32[32,32,20,128]{3,0,2,1:T(8,128)} %copy.13), calls=%async_computation | async-start | bytes 20971520 | tf_op jit(solution)/shard_map/all_to_all | solution.py:21
  38.8 287.0 %all-gather.2.cloned.1.call-start = ((), (), s32[]{:S(2)}) async-start(), calls=%async_computation.1 | async-start | bytes 2621440 | tf_op jit(solution)/shard_map/all_gather | solution.py:12
  325.8 48.2 %copy-start.1 = (s32[1024]{0:T(1024)S(1)}, s32[1024]{0:T(1024)}, u32[]{:S(2)}) copy-start(s32[1024]{0:T(1024)} %param.5) | copy-start | bytes 12292
  374.0 58.8 %slice-start = ((s8[10485760]{0:T(1024)(128)(4,1)}), s8[2097152]{0:T(1024)(128)(4,1)S(1)}, s32[]{:S(2)}) async-start(s8[10485760]{0:T(1024)(128)(4,1)} %bitcast.44), calls=%async_computation.2 | async-start | bytes 4194304
  420.7 12.0 %slice-start.1 = ((s8[10485760]{0:T(1024)(128)(4,1)}), s8[4194304]{0:T(1024)(128)(4,1)S(1)}, s32[]{:S(2)}) async-start(s8[10485760]{0:T(1024)(128)(4,1)} %bitcast.44), calls=%async_computation.3 | async-start | bytes 8388608
  420.7 12.0 %slice-start.2 = ((s8[10485760]{0:T(1024)(128)(4,1)}), s8[4194304]{0:T(1024)(128)(4,1)S(1)}, s32[]{:S(2)}) async-start(s8[10485760]{0:T(1024)(128)(4,1)} %bitcast.44), calls=%async_computation.4 | async-start | bytes 8388608
  420.7 12.0 %copy-start.2 = (bf16[1024,1024]{1,0:T(8,128)(2,1)S(1)}, bf16[1024,1024]{1,0:T(8,128)(2,1)}, u32[]{:S(2)}) copy-start(bf16[1024,1024]{1,0:T(8,128)(2,1)} %all-gather.2.cloned.1.call-done) | copy-start | bytes 6291460
Sparse Core Ops, SparseCore 0:
  41.1 74.9 all-gather.1
where the time goes:
time: 585 us; the launch traced here: 579 us
  waiting for transfers between devices  235 us (40%)
  blocking collectives  158 us (27%)
  local copies, waits for them, and re-layouts  98.1 us (17%)
  matrix products  52.9 us (9%)
  between operations  14.3 us (2%)
  other arithmetic  12.8 us (2%)
  starting transfers between devices  7.86 us (1%)
    all_to_all x1, waiting for transfers between devices, shards(): lax.all_to_all(pieces, ('cls', 'row'), split_axis=1, concat_axis=0, tiled...  235 us
    psum x2, blocking collectives, shards(): lax.psum((jnp.sum(jnp.exp(logits - row_peak[:, None]), axis=1), local_pic...  81.7 us
    pmax x2, blocking collectives, shards(): row_peak = lax.pmax(local_peak, ('cls', 'row'))  76.4 us
    unnamed x14, local copies, waits for them, and re-layouts  33.3 us
    dot_general x2, matrix products, shards(): lax.dot_general(examples, residual, (((0,), (0,)), ((), ())), preferred_e...  29.2 us
    reshape x2, local copies, waits for them, and re-layouts, shards(): pieces = weights.reshape(feature_rows, peer_count, class_count // 128, 128)  24.2 us
    all_to_all x1, local copies, waits for them, and re-layouts, shards(): lax.all_to_all(pieces, ('cls', 'row'), split_axis=1, concat_axis=0, tiled...  17.8 us
    dot_general x1, matrix products, shards(): jnp.dot(examples, current.astype(jnp.bfloat16), preferred_element_type=jn...  12.4 us
  transfers between devices with their start and end apart: 2, of which 1 were waited for; matrix products, arithmetic and copies ran while one was open for 9% of the time, Pallas kernels for 0%

commit v1 on v0

--- a/solution.py
+++ b/solution.py
@@ -40,7 +40,8 @@
         local_picked = jnp.sum(jnp.where(label_hit, logits, 0.0), axis=1)
         row_peak = lax.pmax(local_peak, ("cls", "row"))
         row_total, picked = lax.psum(
-            (jnp.sum(jnp.exp(logits - row_peak[:, None]), axis=1), local_picked), ("cls", "row")
+            lax.psum((jnp.sum(jnp.exp(logits - row_peak[:, None]), axis=1), local_picked), "row"),
+            "cls",
         )
         log_norm = row_peak + jnp.log(row_total)
         loss_rows.append(log_norm - picked)

time: 585 us -> 564 us (0.964)
  local copies, waits for them, and re-layouts: 98.1 us -> 87.6 us
  blocking collectives: 158 us -> 148 us
    psum x2, blocking collectives: 81.7 us -> 16 us  [shards(): lax.psum((jnp.sum(jnp.exp(logits - row_peak[:, None]), axis=1), local_pic...]
    psum x0 -> x2, blocking collectives: none -> 57.9 us  [shards(): lax.psum(lax.psum((jnp.sum(jnp.exp(logits - row_peak[:, None]), axis=1),...]
    unnamed x14, local copies, waits for them, and re-layouts: 33.3 us -> 22.7 us
  transfers between devices with their start and end apart: 2 -> 2, of which waited for: 1 -> 1; matrix products, arithmetic and copies ran while one was open for 9% -> 7% of each run, Pallas kernels for 0% -> 0%
where the time goes in v1:
time: 564 us; the launch traced here: 558 us
  waiting for transfers between devices  234 us (41%)
  blocking collectives  148 us (26%)
  local copies, waits for them, and re-layouts  87.6 us (16%)
  matrix products  52.9 us (9%)
  between operations  14.3 us (3%)
  other arithmetic  12.8 us (2%)
  starting transfers between devices  7.95 us (1%)
    all_to_all x1, waiting for transfers between devices, shards(): lax.all_to_all(pieces, ('cls', 'row'), split_axis=1, concat_axis=0, tiled...  234 us
    pmax x2, blocking collectives, shards(): row_peak = lax.pmax(local_peak, ('cls', 'row'))  73.8 us
    psum x2, blocking collectives, shards(): lax.psum(lax.psum((jnp.sum(jnp.exp(logits - row_peak[:, None]), axis=1),...  57.9 us
    dot_general x2, matrix products, shards(): lax.dot_general(examples, residual, (((0,), (0,)), ((), ())), preferred_e...  29.2 us
    reshape x2, local copies, waits for them, and re-layouts, shards(): pieces = weights.reshape(feature_rows, peer_count, class_count // 128, 128)  24.2 us
    unnamed x14, local copies, waits for them, and re-layouts  22.7 us
    all_to_all x1, local copies, waits for them, and re-layouts, shards(): lax.all_to_all(pieces, ('cls', 'row'), split_axis=1, concat_axis=0, tiled...  17.8 us
    psum x2, blocking collectives, shards(): lax.psum((jnp.sum(jnp.exp(logits - row_peak[:, None]), axis=1), local_pic...  16 us
  transfers between devices with their start and end apart: 2, of which 1 were waited for; matrix products, arithmetic and copies ran while one was open for 7% of the time, Pallas kernels for 0%

profile of v1, /device:TPU:0, one launch (start us, length us, event | category | flops | bytes accessed | tf_op | source)
XLA Modules:
  0.0 557.8 jit_solution(8873525456347711760)
XLA Ops:
  7.2 9.4 %reshape.18 = f32[32,32,20,128]{3,2,1,0:T(8,128)} reshape(f32[32,81920]{1,0:T(8,128)} %param.4) | data formatting | bytes 20971520 | tf_op jit(solution)/shard_map/reshape | solution.py:20
  16.6 14.7 %copy.13 = f32[32,32,20,128]{3,0,2,1:T(8,128)} copy(f32[32,32,20,128]{3,2,1,0:T(8,128)} %reshape.18) | data formatting | bytes 20971520 | tf_op jit(solution)/shard_map/reshape | solution.py:20
  31.3 7.4 %all-to-all-start = ((f32[32,32,20,128]{3,0,2,1:T(8,128)}), f32[32,32,20,128]{3,0,2,1:T(8,128)}, u32[]{:S(2)}, u32[]{:S(2)}) async-start(f32[32,32,20,128]{3,0,2,1:T(8,128)} %copy.13), calls=%async_computation | async-start | bytes 20971520 | tf_op jit(solution)/shard_map/all_to_all | solution.py:21
  38.8 0.5 all-gather.2.cloned.1.call-start
  39.3 0.9 convert_element_type.15
  40.2 234.5 %all-to-all-done = f32[32,32,20,128]{3,0,2,1:T(8,128)} async-done(((f32[32,32,20,128]{3,0,2,1:T(8,128)}), f32[32,32,20,128]{3,0,2,1:T(8,128)}, u32[]{:S(2)}, u32[]{:S(2)}) %all-to-all-start) | async-done | bytes 10485792 | tf_op jit(solution)/shard_map/all_to_all | solution.py:21
  274.7 17.8 %copy.14 = f32[32,32,1,20,128]{4,3,1,0,2:T(8,128)} copy(f32[32,32,1,20,128]{4,1,3,0,2:T(8,128)} %bitcast.1) | data formatting | bytes 20971520 | tf_op jit(solution)/shard_map/all_to_all | solution.py:21
  292.5 11.3 %copy.21 = f32[128,8,20,128]{3,1,2,0:T(8,128)} copy(f32[128,8,20,128]{3,2,1,0:T(8,128)} %bitcast.41) | data formatting | bytes 20971520
  303.9 11.4 %copy.15 = f32[1024,2560]{0,1:T(8,128)} copy(f32[1024,2560]{1,0:T(8,128)} %bitcast.42) | data formatting | bytes 20971520 | tf_op jit(solution)/shard_map/reshape;squeeze | solution.py:30
  315.2 11.4 %fusion.35 = (f32[1024]{0:T(1024)S(1)}, f32[1024,2560]{1,0:T(8,128)}) fusion(bf16[1024,1024]{1,0:T(8,128)(2,1)} %all-gather.2.cloned.1.call-done, f32[1024,2560]{1,0:T(8,128)} %bitcast.43), kind=kOutput, calls=%fused_computation.45 | convolution fusion | flops 5373950976 | bytes 23072768 | tf_op jit(solution)/shard_map/dot_general | solution.py:26
  326.6 36.8 %pmax.14 = f32[1024]{0:T(1024)S(1)} all-reduce(f32[1024]{0:T(1024)S(1)} %get-tuple-element.20), channel_id=1, replica_groups=mesh['cls'=8,'row'=4] {'cls','row'}, use_global_device_ids=true, to_apply=%region_1.2 | all-reduce | flops 1024 | bytes 8192 | tf_op jit(solution)/shard_map/pmax | solution.py:41
  363.4 5.7 %fusion.4 = (f32[1024]{0:T(1024)S(1)}, f32[1024]{0:T(1024)S(1)}) fusion(f32[1024,2560]{1,0:T(8,128)} %get-tuple-element.21, s32[2560]{0:T(1024)S(1)} %iota_add_fusion, s32[1024]{0:T(1024)S(1)} %copy-done.1, f32[1024]{0:T(1024)S(1)} %pmax.14), kind=kLoop, calls=%fused_computation.7 | loop fusion | flops 13105152 | bytes 10512384 | tf_op jit(solution)/shard_map/reduce_sum | solution.py:40
  369.2 5.8 %psum.56 = f32[1024]{0:T(1024)S(1)} all-reduce(f32[1024]{0:T(1024)S(1)} %get-tuple-element.9), channel_id=1, replica_groups=mesh['cls'=8,'row'=4] {'row'}, use_global_device_ids=true, to_apply=%region_3.4 | all-reduce | flops 1024 | bytes 8192 | tf_op jit(solution)/shard_map/psum | solution.py:43
  375.0 21.0 %psum.57 = f32[1024]{0:T(1024)S(1)} all-reduce(f32[1024]{0:T(1024)S(1)} %psum.56), channel_id=1, replica_groups=mesh['cls'=8,'row'=4] {'cls'}, use_global_device_ids=true, to_apply=%region_4.5 | all-reduce | flops 1024 | bytes 8192 | tf_op jit(solution)/shard_map/psum | solution.py:42
  396.1 12.0 %fusion.14 = f32[2560,1024]{1,0:T(8,128)} fusion(bf16[1024,1024]{1,0:T(8,128)(2,1)} %all-gather.2.cloned.1.call-done, f32[1024,2560]{1,0:T(8,128)} %get-tuple-element.21, s32[2560]{0:T(1024)S(1)} %iota_add_fusion, f32[1024]{0:T(1024)S(1)} %log_add_fusion.1, s32[1024]{0:T(1024)S(1)} %copy-done.1), kind=kOutput, calls=%fused_computation.21 | convolution fusion | flops 5381816320 | bytes 23087104 | tf_op jit(solution)/shard_map/dot_general | solution.py:51
  408.1 12.4 %fusion.36 = (f32[1024]{0:T(1024)S(1)}, f32[2560,1024]{1,0:T(8,128)}) fusion(bf16[1024,1024]{1,0:T(8,128)(2,1)S(1)} %copy-done.2, f32[1024,2560]{0,1:T(8,128)S(1)} %bitcast.45, f32[2560,1024]{1,0:T(8,128)} %fusion.14), kind=kOutput, calls=%fused_computation.46 | convolution fusion | flops 5379193856 | bytes 33558528 | tf_op jit(solution)/shard_map/dot_general | solution.py:36
  420.5 37.0 %pmax.15 = f32[1024]{0:T(1024)S(1)} all-reduce(f32[1024]{0:T(1024)S(1)} %get-tuple-element.22), channel_id=1, replica_groups=mesh['cls'=8,'row'=4] {'cls','row'}, use_global_device_ids=true, to_apply=%region_6.7 | all-reduce | flops 1024 | bytes 8192 | tf_op jit(solution)/shard_map/pmax | solution.py:41
  457.5 11.5 %copy.16 = f32[2560,1024]{0,1:T(8,128)} copy(f32[2560,1024]{1,0:T(8,128)} %get-tuple-element.23) | data formatting | bytes 20971520 | tf_op jit(solution)/shard_map/dot_general | solution.py:36
  469.0 5.6 %fusion.5 = (f32[1024]{0:T(1024)S(1)}, f32[1024]{0:T(1024)S(1)}) fusion(f32[2560,1024]{0,1:T(8,128)} %copy.16, s32[2560]{0:T(1024)S(1)} %iota_add_fusion, s32[1024]{0:T(1024)S(1)} %copy-done.1, f32[1024]{0:T(1024)S(1)} %pmax.15), kind=kLoop, calls=%fused_computation.8 | loop fusion | flops 13105152 | bytes 10512384 | tf_op jit(solution)/shard_map/reduce_sum | solution.py:40
  474.6 10.1 %all-reduce.1 = (f32[1024]{0:T(1024)S(1)}, f32[1024]{0:T(1024)S(1)}, f32[1024]{0:T(1024)S(1)}) all-reduce(f32[1024]{0:T(1024)S(1)} %get-tuple-element.11, f32[1024]{0:T(1024)S(1)} %get-tuple-element.10, f32[1024]{0:T(1024)S(1)} %get-tuple-element.8), channel_id=1, replica_groups=mesh['cls'=8,'row'=4] {'row'}, use_global_device_ids=true, to_apply=%region_8.9 | all-reduce | flops 3072 | bytes 24576 | tf_op jit(solution)/shard_map/psum | solution.py:43
  484.7 36.8 %all-reduce = (f32[1024]{0:T(1024)S(1)}, f32[1024]{0:T(1024)S(1)}, f32[1024]{0:T(1024)S(1)}) all-reduce(f32[1024]{0:T(1024)S(1)} %get-tuple-element.15, f32[1024]{0:T(1024)S(1)} %get-tuple-element.16, f32[1024]{0:T(1024)S(1)} %get-tuple-element.17), channel_id=1, replica_groups=mesh['cls'=8,'row'=4] {'cls'}, use_global_device_ids=true, to_apply=%region_9.10 | all-reduce | flops 3072 | bytes 24576 | tf_op jit(solution)/shard_map/psum | solution.py:42
  521.5 17.2 %fusion.6 = f32[1024,2560]{0,1:T(8,128)} fusion(f32[1024,2560]{0,1:T(8,128)} %copy.15, f32[2560,1024]{1,0:T(8,128)} %fusion.14, bf16[1024,1024]{1,0:T(8,128)(2,1)} %all-gather.2.cloned.1.call-done, f32[2560,1024]{0,1:T(8,128)} %copy.16, f32[1024]{0:T(1024)S(1)} %get-tuple-element.19, s32[2560]{0:T(1024)S(1)} %iota_add_fusion, s32[1024]{0:T(1024)S(1)} %copy-done.1), kind=kOutput, calls=%fused_computation.11 | convolution fusion | flops 5394923520 | bytes 44058624 | tf_op jit(solution)/shard_map/dot_general | solution.py:51
  538.7 11.4 %copy.18 = f32[1024,2560]{1,0:T(8,128)} copy(f32[1024,2560]{0,1:T(8,128)} %fusion.6) | data formatting | bytes 20971520
  550.1 0.6 pad_maximum_fusion
  (19 shorter events, 0.1 us)
Async XLA Ops:
  31.3 8.0 %copy-start = (f32[256,1024]{1,0:T(8,128)S(1)}, f32[256,1024]{1,0:T(8,128)}, u32[]{:S(2)}) copy-start(f32[256,1024]{1,0:T(8,128)} %param.3) | copy-start | bytes 3145732
  31.3 243.4 %all-to-all-start = ((f32[32,32,20,128]{3,0,2,1:T(8,128)}), f32[32,32,20,128]{3,0,2,1:T(8,128)}, u32[]{:S(2)}, u32[]{:S(2)}) async-start(f32[32,32,20,128]{3,0,2,1:T(8,128)} %copy.13), calls=%async_computation | async-start | bytes 20971520 | tf_op jit(solution)/shard_map/all_to_all | solution.py:21
  38.8 276.5 %all-gather.2.cloned.1.call-start = ((), (), s32[]{:S(2)}) async-start(), calls=%async_computation.1 | async-start | bytes 2621440 | tf_op jit(solution)/shard_map/all_gather | solution.py:12
  315.2 48.2 %copy-start.1 = (s32[1024]{0:T(1024)S(1)}, s32[1024]{0:T(1024)}, u32[]{:S(2)}) copy-start(s32[1024]{0:T(1024)} %param.5) | copy-start | bytes 12292
  363.4 44.7 %slice-start = ((s8[10485760]{0:T(1024)(128)(4,1)}), s8[2097152]{0:T(1024)(128)(4,1)S(1)}, s32[]{:S(2)}) async-start(s8[10485760]{0:T(1024)(128)(4,1)} %bitcast.44), calls=%async_computation.2 | async-start | bytes 4194304
  396.0 12.0 %slice-start.1 = ((s8[10485760]{0:T(1024)(128)(4,1)}), s8[4194304]{0:T(1024)(128)(4,1)S(1)}, s32[]{:S(2)}) async-start(s8[10485760]{0:T(1024)(128)(4,1)} %bitcast.44), calls=%async_computation.3 | async-start | bytes 8388608
  396.1 12.0 %slice-start.2 = ((s8[10485760]{0:T(1024)(128)(4,1)}), s8[4194304]{0:T(1024)(128)(4,1)S(1)}, s32[]{:S(2)}) async-start(s8[10485760]{0:T(1024)(128)(4,1)} %bitcast.44), calls=%async_computation.4 | async-start | bytes 8388608
  396.1 12.0 %copy-start.2 = (bf16[1024,1024]{1,0:T(8,128)(2,1)S(1)}, bf16[1024,1024]{1,0:T(8,128)(2,1)}, u32[]{:S(2)}) copy-start(bf16[1024,1024]{1,0:T(8,128)(2,1)} %all-gather.2.cloned.1.call-done) | copy-start | bytes 6291460
Sparse Core Ops, SparseCore 0:
  41.1 74.9 all-gather.1
